TPU v7x, 256 devices: a 4x2x16 block of a 4x16x16 slice. The times are simulated.
256 devices in a mesh: groups: 2 (over y), expert: 16 (over z), hidden: 8 (over x, core).
Axes of the slice: x: 4, y: 2, z: 16, core: 2. Of those that a mesh axis runs over, the one named last changes fastest.
The devices are a block of a 4x16x16 slice.
Arguments:
- tokens: bfloat16 [256, 196, 1024], P(('groups', 'expert', 'hidden')), parts along dimension 0, may hold values from -40 to 40
- slot_params: bfloat16 [2048, 64], P('groups'), parts along dimension 0, may hold values from -0.75 to 0.75
- expert_up: bfloat16 [128, 1024, 4096], P(('groups', 'expert'), None, 'hidden'), parts along dimension 0, may hold values from -0.1875 to 0.1875
- expert_down: bfloat16 [128, 4096, 1024], P(('groups', 'expert'), 'hidden'), parts along dimension 0, may hold values from -0.09375 to 0.09375
- cotangent: bfloat16 [256, 196, 1024], P(('groups', 'expert', 'hidden')), parts along dimension 0, may hold values from -6 to 6
Outputs:
- mixed: bfloat16 [256, 196, 1024], P(('groups', 'expert', 'hidden')), parts along dimension 0
- d_tokens: bfloat16 [256, 196, 1024], P(('groups', 'expert', 'hidden')), parts along dimension 0
- d_slot_params: float32 [2048, 64], P('groups'), parts along dimension 0
There are 2 independent parts, one for each index of `groups`. A program takes and returns all parts, laid end to end along the dimension named above; each array names one. Nothing has to cross between parts.
All inputs are finite; a program needn't handle non-finite values.
Results may differ from a plain program's by a relative error of at most 0.0077.
Values may be sent and summed in bfloat16 or wider, within the bound.
A program may use at most 64 MiB of HBM per device.

v0:
```python
import jax
import jax.numpy as jnp
from jax import lax
from jax.sharding import Mesh
from jax.sharding import PartitionSpec as P

HIDDEN = ("hidden_0", "hidden_1")
GROUPS_EXPERT_HIDDEN = ("groups", "expert", "hidden_0", "hidden_1")


inv_root_two = 0.7071067811865476
inv_root_tau = 0.3989422804014327


def in_order(blocks, dim):
    blocks = jnp.moveaxis(blocks, 0, dim)
    dims = blocks.shape
    return blocks.reshape(*dims[:dim], dims[dim] * dims[dim + 1], *dims[dim + 2 :])


def from_everyone(x, axis):
    copies = jnp.broadcast_to(x, (lax.axis_size(axis), *x.shape))
    return lax.all_to_all(copies, axis, split_axis=0, concat_axis=0, tiled=True)


def gather_directly(x, axis, dim):
    return in_order(from_everyone(x, axis), dim)


def in_blocks(x, dim, devices):
    dims = x.shape
    blocks = x.reshape(*dims[:dim], devices, dims[dim] // devices, *dims[dim + 1 :])
    return jnp.moveaxis(blocks, dim, 0)


def summed_on_arrival(x, axis, dim):
    blocks = in_blocks(x, dim, lax.axis_size(axis))
    arrived = lax.all_to_all(blocks, axis, split_axis=0, concat_axis=0, tiled=True)
    return arrived.sum(axis=0)


def summed_rows(x, axes, dim):
    far, near = axes
    own = summed_on_arrival(in_blocks(x, dim, lax.axis_size(far)), near, dim + 1)
    return jnp.sum(lax.all_to_all(own, far, 0, 0, tiled=True), axis=0)


def filled_up(lines, devices):
    spare = -len(lines) % devices
    return jnp.pad(lines, [(0, spare)] + [(0, 0)] * (lines.ndim - 1))


def whole_of(x, axes, dim):
    far, near = axes
    blocks = from_everyone(from_everyone(x, far), near)
    return in_order(blocks.swapaxes(0, 1).reshape(-1, *x.shape), dim)


def nested_sum(x, axes):
    lines = x.reshape(-1, x.shape[-1])
    own = summed_rows(filled_up(lines, lax.axis_size(axes[0]) * lax.axis_size(axes[1])), axes, 0)
    whole = whole_of(own, axes, 0)
    return whole[: len(lines)].reshape(x.shape)


def gelu_exact(value):
    return 0.5 * value * (1.0 + lax.erf(value * inv_root_two))


def gelu_slope(value):
    return (
        0.5 * (1.0 + lax.erf(value * inv_root_two))
        + value * jnp.exp(-0.5 * value * value) * inv_root_tau
    )


def per_device(tokens, slot_params, expert_up, expert_down, cotangent):
    img_count, seq_length, model_width = tokens.shape
    slot_count = slot_params.shape[1]
    expert_count = lax.axis_size("expert")
    hidden_count = lax.axis_size(HIDDEN)
    local_experts = expert_up.shape[0]
    group_slots = slot_count // expert_count
    per_expert = group_slots // local_experts

    def expand(row_block):
        grouped = row_block.reshape(row_block.shape[0], local_experts, per_expert, model_width)
        return jnp.einsum("iesd,edf->iesf", grouped, expert_up, preferred_element_type=jnp.float32)

    def shrink(act_block):
        result = jnp.einsum(
            "iesf,efd->iesd", act_block, expert_down, preferred_element_type=jnp.float32
        )
        return result.reshape(act_block.shape[0], group_slots, model_width)

    def back_hidden(grad_block, pre_block):
        grouped = grad_block.reshape(grad_block.shape[0], local_experts, per_expert, model_width)
        slope_in = jnp.einsum(
            "iesd,efd->iesf", grouped, expert_down, preferred_element_type=jnp.float32
        )
        return (slope_in * gelu_slope(pre_block)).astype(jnp.bfloat16)

    def back_in(dpre_block):
        result = jnp.einsum(
            "iesf,edf->iesd", dpre_block, expert_up, preferred_element_type=jnp.float32
        )
        return result.reshape(dpre_block.shape[0], group_slots, model_width)

    def send_sectioned(slot_block, row_fn):
        parted = lax.all_to_all(slot_block, "expert", split_axis=1, concat_axis=0, tiled=True)
        return row_fn(gather_directly(parted, HIDDEN, 0), jnp.int32(0))

    def sum_sectioned(term_fn, total_rows):
        summed = summed_on_arrival(
            term_fn(jnp.int32(0), total_rows // hidden_count * lax.axis_size(HIDDEN)), HIDDEN, 0
        )
        return lax.all_to_all(
            summed.astype(jnp.bfloat16), "expert", split_axis=0, concat_axis=1, tiled=True
        )

    logits = jnp.einsum("imd,ds->ims", tokens, slot_params, preferred_element_type=jnp.float32)
    dispatch = jax.nn.softmax(logits, axis=1)
    combine = jax.nn.softmax(logits, axis=2)
    dispatch_half = dispatch.astype(jnp.bfloat16)
    combine_half = combine.astype(jnp.bfloat16)
    slots_in = jnp.einsum(
        "ims,imd->isd", dispatch_half, tokens, preferred_element_type=jnp.float32
    ).astype(jnp.bfloat16)
    pre_act = send_sectioned(slots_in, lambda shard_rows, first_row: expand(shard_rows))
    activated = gelu_exact(pre_act).astype(jnp.bfloat16)

    def down_terms(first_row, row_total):
        return shrink(activated)

    slots_out = sum_sectioned(down_terms, activated.shape[0])
    mixed = jnp.einsum(
        "ims,isd->imd", combine_half, slots_out, preferred_element_type=jnp.float32
    ).astype(jnp.bfloat16)
    d_combine = jnp.einsum("imd,isd->ims", cotangent, slots_out, preferred_element_type=jnp.float32)
    grad_combine = (
        combine * (d_combine - jnp.sum(combine * d_combine, axis=2, keepdims=True))
    ).astype(jnp.bfloat16)
    d_slots_out = jnp.einsum(
        "ims,imd->isd", combine_half, cotangent, preferred_element_type=jnp.float32
    ).astype(jnp.bfloat16)

    def grad_rows(shard_rows, first_row):
        return back_hidden(shard_rows, pre_act)

    d_pre = send_sectioned(d_slots_out, grad_rows)

    def input_terms(first_row, row_total):
        return back_in(d_pre)

    d_slots_in = sum_sectioned(input_terms, d_pre.shape[0])
    d_dispatch = jnp.einsum("imd,isd->ims", tokens, d_slots_in, preferred_element_type=jnp.float32)
    grad_dispatch = (
        dispatch * (d_dispatch - jnp.sum(dispatch * d_dispatch, axis=1, keepdims=True))
    ).astype(jnp.bfloat16)
    d_tokens = jnp.einsum(
        "ims,isd->imd", dispatch_half, d_slots_in, preferred_element_type=jnp.float32
    )
    d_tokens = d_tokens + jnp.einsum(
        "ims,ds->imd", grad_combine, slot_params, preferred_element_type=jnp.float32
    )
    d_tokens = d_tokens + jnp.einsum(
        "ims,ds->imd", grad_dispatch, slot_params, preferred_element_type=jnp.float32
    )
    dispatch_term = jnp.einsum(
        "imd,ims->ds", tokens, grad_dispatch, preferred_element_type=jnp.float32
    )
    combine_term = jnp.einsum(
        "imd,ims->ds", tokens, grad_combine, preferred_element_type=jnp.float32
    )
    d_slot_params = nested_sum(combine_term + dispatch_term, (("expert", "hidden_0"), "hidden_1"))
    return (mixed, d_tokens.astype(jnp.bfloat16), d_slot_params)


def solution(mesh):
    split = Mesh(
        mesh.devices.reshape(mesh.shape["groups"], mesh.shape["expert"], 4, 2),
        ("groups", "expert", "hidden_0", "hidden_1"),
    )
    return jax.shard_map(
        per_device,
        mesh=split,
        in_specs=(
            P(GROUPS_EXPERT_HIDDEN, None, None),
            P("groups", None),
            P(("groups", "expert"), None, HIDDEN),
            P(("groups", "expert"), HIDDEN, None),
            P(GROUPS_EXPERT_HIDDEN, None, None),
        ),
        out_specs=(
            P(GROUPS_EXPERT_HIDDEN, None, None),
            P(GROUPS_EXPERT_HIDDEN, None, None),
            P("groups", None),
        ),
        check_vma=False,
    )
```

profile of v0, /device:TPU:33, one launch (start us, length us, event | category | flops | bytes accessed | tf_op | source)
XLA Modules:
  0.0 269.8 jit_solution(6770022749136223080)
XLA Ops:
  6.8 24.5 %all-to-all-start = ((bf16[16,2,2048]{2,1,0:T(2,128)(2,1)}), bf16[16,2,2048]{2,1,0:T(2,128)(2,1)S(1)}, u32[]{:S(2)}, u32[]{:S(2)}) async-start(bf16[16,2,2048]{2,1,0:T(2,128)(2,1)} %reshape.146), calls=%async_computation | async-start | bytes 262144 | tf_op jit(solution)/shard_map/all_to_all | solution.py:110
  34.9 8.2 %all-to-all-done = bf16[16,2,2048]{2,1,0:T(2,128)(2,1)S(1)} async-done(((bf16[16,2,2048]{2,1,0:T(2,128)(2,1)}), bf16[16,2,2048]{2,1,0:T(2,128)(2,1)S(1)}, u32[]{:S(2)}, u32[]{:S(2)}) %all-to-all-start) | async-done | bytes 131104 | tf_op jit(solution)/shard_map/all_to_all | solution.py:110
  43.1 6.2 %all-to-all-start.4 = ((bf16[16,2,2048]{2,1,0:T(2,128)(2,1)}), bf16[16,2,2048]{2,1,0:T(2,128)(2,1)S(1)}, u32[]{:S(2)}, u32[]{:S(2)}) async-start(bf16[16,2,2048]{2,1,0:T(2,128)(2,1)} %reshape.148), calls=%async_computation.4 | async-start | bytes 262144 | tf_op jit(solution)/shard_map/all_to_all | solution.py:110
  50.3 10.8 %all-to-all-done.4 = bf16[16,2,2048]{2,1,0:T(2,128)(2,1)S(1)} async-done(((bf16[16,2,2048]{2,1,0:T(2,128)(2,1)}), bf16[16,2,2048]{2,1,0:T(2,128)(2,1)S(1)}, u32[]{:S(2)}, u32[]{:S(2)}) %all-to-all-start.4) | async-done | bytes 131104 | tf_op jit(solution)/shard_map/all_to_all | solution.py:110
  62.2 8.4 %all-to-all-start.1 = ((bf16[8,16,4,1024]{3,1,2,0:T(8,128)(2,1)}), bf16[8,16,4,1024]{3,1,2,0:T(8,128)(2,1)S(1)}, u32[]{:S(2)}, u32[]{:S(2)}) async-start(bf16[8,16,4,1024]{3,1,2,0:T(8,128)(2,1)} %broadcast_in_dim.8), calls=%async_computation.1 | async-start | bytes 2097152 | tf_op jit(solution)/shard_map/all_to_all | solution.py:23
  71.6 14.0 %all-to-all-done.1 = bf16[8,16,4,1024]{3,1,2,0:T(8,128)(2,1)S(1)} async-done(((bf16[8,16,4,1024]{3,1,2,0:T(8,128)(2,1)}), bf16[8,16,4,1024]{3,1,2,0:T(8,128)(2,1)S(1)}, u32[]{:S(2)}, u32[]{:S(2)}) %all-to-all-start.1) | async-done | bytes 1048608 | tf_op jit(solution)/shard_map/all_to_all | solution.py:23
  86.7 5.1 %all-to-all-start.5 = ((bf16[8,16,4,1024]{3,1,2,0:T(8,128)(2,1)}), bf16[8,16,4,1024]{3,1,2,0:T(8,128)(2,1)}, u32[]{:S(2)}, u32[]{:S(2)}) async-start(bf16[8,16,4,1024]{3,1,2,0:T(8,128)(2,1)} %broadcast_in_dim.9), calls=%async_computation.5 | async-start | bytes 2097152 | tf_op jit(solution)/shard_map/all_to_all | solution.py:23
  97.6 9.4 %all-to-all-done.5 = bf16[8,16,4,1024]{3,1,2,0:T(8,128)(2,1)} async-done(((bf16[8,16,4,1024]{3,1,2,0:T(8,128)(2,1)}), bf16[8,16,4,1024]{3,1,2,0:T(8,128)(2,1)}, u32[]{:S(2)}, u32[]{:S(2)}) %all-to-all-start.5) | async-done | bytes 1048608 | tf_op jit(solution)/shard_map/all_to_all | solution.py:23
  106.9 4.5 %all-to-all-start.2 = ((f32[8,16,4,1024]{3,1,2,0:T(8,128)}), f32[8,16,4,1024]{3,1,2,0:T(8,128)S(1)}, u32[]{:S(2)}, u32[]{:S(2)}) async-start(f32[8,16,4,1024]{3,1,2,0:T(8,128)} %copy.63), calls=%async_computation.2 | async-start | bytes 4194304 | tf_op jit(solution)/shard_map/all_to_all | solution.py:38
  113.7 8.0 %fusion.9 = f32[4,128,1024]{2,1,0:T(8,128)} fusion(bf16[4,1024,512]{2,1,0:T(8,128)(2,1)} %param.7, bf16[128,4,1024]{2,0,1:T(8,128)(2,1)} %bitcast.110, bf16[4,512,1024]{2,1,0:T(8,128)(2,1)} %param.8, f32[128,4,1,512]{3,0,1,2:T(8,128)S(1)} %convolution_bitcast_fusion.1), kind=kOutput, calls=%fused_computation.20 | convolution fusion | flops 1076363264 | bytes 12582912 | tf_op jit(solution)/shard_map/iesf,edf->iesd/dot_general | solution.py:104
  121.7 3.1 %copy.69 = f32[8,16,4,1024]{3,1,2,0:T(8,128)} copy(f32[8,16,4,1024]{3,1,0,2:T(8,128)} %bitcast.108) | data formatting | bytes 4194304 | tf_op jit(solution)/shard_map/reshape;reshape | solution.py:32
  124.9 12.8 %all-to-all-done.2 = f32[8,16,4,1024]{3,1,2,0:T(8,128)S(1)} async-done(((f32[8,16,4,1024]{3,1,2,0:T(8,128)}), f32[8,16,4,1024]{3,1,2,0:T(8,128)S(1)}, u32[]{:S(2)}, u32[]{:S(2)}) %all-to-all-start.2) | async-done | bytes 2097184 | tf_op jit(solution)/shard_map/all_to_all | solution.py:38
  137.7 5.2 %all-to-all-start.6 = ((f32[8,16,4,1024]{3,1,2,0:T(8,128)}), f32[8,16,4,1024]{3,1,2,0:T(8,128)}, u32[]{:S(2)}, u32[]{:S(2)}) async-start(f32[8,16,4,1024]{3,1,2,0:T(8,128)} %copy.69), calls=%async_computation.6 | async-start | bytes 4194304 | tf_op jit(solution)/shard_map/all_to_all | solution.py:38
  143.8 25.5 %all-to-all-done.6 = f32[8,16,4,1024]{3,1,2,0:T(8,128)} async-done(((f32[8,16,4,1024]{3,1,2,0:T(8,128)}), f32[8,16,4,1024]{3,1,2,0:T(8,128)}, u32[]{:S(2)}, u32[]{:S(2)}) %all-to-all-start.6) | async-done | bytes 2097184 | tf_op jit(solution)/shard_map/all_to_all | solution.py:38
  169.3 4.0 %all-to-all-start.3 = ((bf16[16,4,1024]{2,1,0:T(4,128)(2,1)}), bf16[16,4,1024]{2,1,0:T(4,128)(2,1)S(1)}, u32[]{:S(2)}, u32[]{:S(2)}) async-start(bf16[16,4,1024]{2,1,0:T(4,128)(2,1)} %copy.65), calls=%async_computation.3 | async-start | bytes 262144 | tf_op jit(solution)/shard_map/all_to_all | solution.py:117
  175.8 9.1 %all-to-all-done.3 = bf16[16,4,1024]{2,1,0:T(4,128)(2,1)S(1)} async-done(((bf16[16,4,1024]{2,1,0:T(4,128)(2,1)}), bf16[16,4,1024]{2,1,0:T(4,128)(2,1)S(1)}, u32[]{:S(2)}, u32[]{:S(2)}) %all-to-all-start.3) | async-done | bytes 131104 | tf_op jit(solution)/shard_map/all_to_all | solution.py:117
  184.9 5.8 %all-to-all-start.7 = ((bf16[16,4,1024]{2,1,0:T(4,128)(2,1)}), bf16[16,4,1024]{2,1,0:T(4,128)(2,1)S(1)}, u32[]{:S(2)}, u32[]{:S(2)}) async-start(bf16[16,4,1024]{2,1,0:T(4,128)(2,1)} %copy.71), calls=%async_computation.7 | async-start | bytes 262144 | tf_op jit(solution)/shard_map/all_to_all | solution.py:117
  191.0 11.5 %all-to-all-done.7 = bf16[16,4,1024]{2,1,0:T(4,128)(2,1)S(1)} async-done(((bf16[16,4,1024]{2,1,0:T(4,128)(2,1)}), bf16[16,4,1024]{2,1,0:T(4,128)(2,1)S(1)}, u32[]{:S(2)}, u32[]{:S(2)}) %all-to-all-start.7) | async-done | bytes 131104 | tf_op jit(solution)/shard_map/all_to_all | solution.py:117
  204.0 7.6 %all_to_all.82 = f32[2,1,32768]{2,1,0:T(1,128)S(1)} all-to-all(f32[2,1,32768]{2,1,0:T(1,128)S(1)} %reshape.150), channel_id=1, replica_groups=mesh['groups'=2,'expert'=16,'hidden_0'=4,'hidden_1'=2] {'hidden_1'}, dimensions={0} | all-to-all | bytes 524288 | tf_op jit(solution)/shard_map/all_to_all | solution.py:38
  214.9 6.5 %all-to-all-start.9 = ((f32[64,1,512]{2,1,0:T(1,128)}), f32[64,1,512]{2,1,0:T(1,128)S(1)}, u32[]{:S(2)}, u32[]{:S(2)}) async-start(f32[64,1,512]{2,1,0:T(1,128)} %reshape.152), calls=%async_computation.9 | async-start | bytes 262144 | tf_op jit(solution)/shard_map/all_to_all | solution.py:45
  221.8 13.5 %all-to-all-done.9 = f32[64,1,512]{2,1,0:T(1,128)S(1)} async-done(((f32[64,1,512]{2,1,0:T(1,128)}), f32[64,1,512]{2,1,0:T(1,128)S(1)}, u32[]{:S(2)}, u32[]{:S(2)}) %all-to-all-start.9) | async-done | bytes 131104 | tf_op jit(solution)/shard_map/all_to_all | solution.py:45
  237.3 7.6 %all-to-all-start.10 = ((f32[64,1,512]{2,1,0:T(1,128)}), f32[64,1,512]{2,1,0:T(1,128)S(1)}, u32[]{:S(2)}, u32[]{:S(2)}) async-start(f32[64,1,512]{2,1,0:T(1,128)} %reshape.154), calls=%async_computation.10 | async-start | bytes 262144 | tf_op jit(solution)/shard_map/all_to_all | solution.py:23
  247.4 11.1 %all-to-all-done.10 = f32[64,1,512]{2,1,0:T(1,128)S(1)} async-done(((f32[64,1,512]{2,1,0:T(1,128)}), f32[64,1,512]{2,1,0:T(1,128)S(1)}, u32[]{:S(2)}, u32[]{:S(2)}) %all-to-all-start.10) | async-done | bytes 131104 | tf_op jit(solution)/shard_map/all_to_all | solution.py:23
  260.0 7.1 %all_to_all.83 = f32[2,1,32768]{2,1,0:T(1,128)S(1)} all-to-all(f32[2,1,32768]{2,1,0:T(1,128)S(1)} %reshape.156), channel_id=1, replica_groups=mesh['groups'=2,'expert'=16,'hidden_0'=4,'hidden_1'=2] {'hidden_1'}, dimensions={0} | all-to-all | bytes 524288 | tf_op jit(solution)/shard_map/all_to_all | solution.py:23
  (90 shorter events, 39.4 us)
Async XLA Ops:
  0.6 1.0 copy-start
  2.9 0.5 copy-start.8
  2.9 29.8 %copy-start.6 = (f32[196]{0:T(256)}, f32[196]{0:T(256)S(1)}, u32[]{:S(2)}) copy-start(f32[196]{0:T(256)S(1)} %get-tuple-element.22) | copy-start | bytes 2356
  2.9 59.3 %copy-start.2 = (f32[196,64]{0,1:T(8,128)}, f32[196,64]{0,1:T(8,128)S(1)}, u32[]{:S(2)}) copy-start(f32[196,64]{0,1:T(8,128)S(1)} %get-tuple-element.24) | copy-start | bytes 150532
  3.1 0.6 copy-start.12
  3.1 29.6 %copy-start.10 = (f32[196]{0:T(256)}, f32[196]{0:T(256)S(1)}, u32[]{:S(2)}) copy-start(f32[196]{0:T(256)S(1)} %get-tuple-element.20) | copy-start | bytes 2356
  6.8 36.3 %all-to-all-start = ((bf16[16,2,2048]{2,1,0:T(2,128)(2,1)}), bf16[16,2,2048]{2,1,0:T(2,128)(2,1)S(1)}, u32[]{:S(2)}, u32[]{:S(2)}) async-start(bf16[16,2,2048]{2,1,0:T(2,128)(2,1)} %reshape.146), calls=%async_computation | async-start | bytes 262144 | tf_op jit(solution)/shard_map/all_to_all | solution.py:110
  43.1 18.0 %all-to-all-start.4 = ((bf16[16,2,2048]{2,1,0:T(2,128)(2,1)}), bf16[16,2,2048]{2,1,0:T(2,128)(2,1)S(1)}, u32[]{:S(2)}, u32[]{:S(2)}) async-start(bf16[16,2,2048]{2,1,0:T(2,128)(2,1)} %reshape.148), calls=%async_computation.4 | async-start | bytes 262144 | tf_op jit(solution)/shard_map/all_to_all | solution.py:110
  62.2 23.3 %all-to-all-start.1 = ((bf16[8,16,4,1024]{3,1,2,0:T(8,128)(2,1)}), bf16[8,16,4,1024]{3,1,2,0:T(8,128)(2,1)S(1)}, u32[]{:S(2)}, u32[]{:S(2)}) async-start(bf16[8,16,4,1024]{3,1,2,0:T(8,128)(2,1)} %broadcast_in_dim.8), calls=%async_computation.1 | async-start | bytes 2097152 | tf_op jit(solution)/shard_map/all_to_all | solution.py:23
  86.7 20.3 %all-to-all-start.5 = ((bf16[8,16,4,1024]{3,1,2,0:T(8,128)(2,1)}), bf16[8,16,4,1024]{3,1,2,0:T(8,128)(2,1)}, u32[]{:S(2)}, u32[]{:S(2)}) async-start(bf16[8,16,4,1024]{3,1,2,0:T(8,128)(2,1)} %broadcast_in_dim.9), calls=%async_computation.5 | async-start | bytes 2097152 | tf_op jit(solution)/shard_map/all_to_all | solution.py:23
  91.9 3.5 %copy-start.1 = (bf16[4,512,1024]{2,1,0:T(8,128)(2,1)S(1)}, bf16[4,512,1024]{2,1,0:T(8,128)(2,1)}, u32[]{:S(2)}) copy-start(bf16[4,512,1024]{2,1,0:T(8,128)(2,1)} %param.8) | copy-start | bytes 12582916
  106.9 30.8 %all-to-all-start.2 = ((f32[8,16,4,1024]{3,1,2,0:T(8,128)}), f32[8,16,4,1024]{3,1,2,0:T(8,128)S(1)}, u32[]{:S(2)}, u32[]{:S(2)}) async-start(f32[8,16,4,1024]{3,1,2,0:T(8,128)} %copy.63), calls=%async_computation.2 | async-start | bytes 4194304 | tf_op jit(solution)/shard_map/all_to_all | solution.py:38
  124.9 65.9 %copy-start.4 = (bf16[1,196,1024]{2,1,0:T(8,128)(2,1)S(1)}, bf16[1,196,1024]{2,1,0:T(8,128)(2,1)}, u32[]{:S(2)}) copy-start(bf16[1,196,1024]{2,1,0:T(8,128)(2,1)} %param.9) | copy-start | bytes 1204228
  137.7 31.6 %all-to-all-start.6 = ((f32[8,16,4,1024]{3,1,2,0:T(8,128)}), f32[8,16,4,1024]{3,1,2,0:T(8,128)}, u32[]{:S(2)}, u32[]{:S(2)}) async-start(f32[8,16,4,1024]{3,1,2,0:T(8,128)} %copy.69), calls=%async_computation.6 | async-start | bytes 4194304 | tf_op jit(solution)/shard_map/all_to_all | solution.py:38
  142.9 59.6 %copy-start.3 = (f32[196,64]{0,1:T(8,128)S(1)}, f32[196,64]{0,1:T(8,128)}, u32[]{:S(2)}) copy-start(f32[196,64]{0,1:T(8,128)} %copy-done.2) | copy-start | bytes 150532
  142.9 59.7 %copy-start.7 = (f32[196]{0:T(256)S(1)}, f32[196]{0:T(256)}, u32[]{:S(2)}) copy-start(f32[196]{0:T(256)} %copy-done.6) | copy-start | bytes 2356
  142.9 59.7 %copy-start.9 = (f32[64]{0:T(128)S(1)}, f32[64]{0:T(128)}, u32[]{:S(2)}) copy-start(f32[64]{0:T(128)} %copy-done.8) | copy-start | bytes 772
  142.9 59.7 %copy-start.11 = (f32[196]{0:T(256)S(1)}, f32[196]{0:T(256)}, u32[]{:S(2)}) copy-start(f32[196]{0:T(256)} %copy-done.10) | copy-start | bytes 2356
  142.9 59.7 %copy-start.13 = (f32[64]{0:T(128)S(1)}, f32[64]{0:T(128)}, u32[]{:S(2)}) copy-start(f32[64]{0:T(128)} %copy-done.12) | copy-start | bytes 772
  169.3 15.6 %all-to-all-start.3 = ((bf16[16,4,1024]{2,1,0:T(4,128)(2,1)}), bf16[16,4,1024]{2,1,0:T(4,128)(2,1)S(1)}, u32[]{:S(2)}, u32[]{:S(2)}) async-start(bf16[16,4,1024]{2,1,0:T(4,128)(2,1)} %copy.65), calls=%async_computation.3 | async-start | bytes 262144 | tf_op jit(solution)/shard_map/all_to_all | solution.py:117
  184.9 17.6 %all-to-all-start.7 = ((bf16[16,4,1024]{2,1,0:T(4,128)(2,1)}), bf16[16,4,1024]{2,1,0:T(4,128)(2,1)S(1)}, u32[]{:S(2)}, u32[]{:S(2)}) async-start(bf16[16,4,1024]{2,1,0:T(4,128)(2,1)} %copy.71), calls=%async_computation.7 | async-start | bytes 262144 | tf_op jit(solution)/shard_map/all_to_all | solution.py:117
  203.6 42.3 %copy-start.5 = (bf16[1024,64]{0,1:T(8,128)(2,1)S(1)}, bf16[1024,64]{0,1:T(8,128)(2,1)}, u32[]{:S(2)}) copy-start(bf16[1024,64]{0,1:T(8,128)(2,1)} %param.6) | copy-start | bytes 393220
  214.9 20.3 %all-to-all-start.9 = ((f32[64,1,512]{2,1,0:T(1,128)}), f32[64,1,512]{2,1,0:T(1,128)S(1)}, u32[]{:S(2)}, u32[]{:S(2)}) async-start(f32[64,1,512]{2,1,0:T(1,128)} %reshape.152), calls=%async_computation.9 | async-start | bytes 262144 | tf_op jit(solution)/shard_map/all_to_all | solution.py:45
  237.3 21.2 %all-to-all-start.10 = ((f32[64,1,512]{2,1,0:T(1,128)}), f32[64,1,512]{2,1,0:T(1,128)S(1)}, u32[]{:S(2)}, u32[]{:S(2)}) async-start(f32[64,1,512]{2,1,0:T(1,128)} %reshape.154), calls=%async_computation.10 | async-start | bytes 262144 | tf_op jit(solution)/shard_map/all_to_all | solution.py:23
where the time goes:
time: 271 us; the launch traced here: 270 us
  waiting for transfers between devices  126 us (46%)
  starting transfers between devices  77.7 us (29%)
  local copies, waits for them, and re-layouts  22.1 us (8%)
  matrix products  18.4 us (7%)
  blocking collectives  14.7 us (5%)
  other arithmetic  9.97 us (4%)
    all_to_all x2, waiting for transfers between devices, summed_on_arrival(): lax.all_to_all(blocks, axis, split_axis=0, concat_axis=0, tiled=True)  38.3 us
    all_to_all x3, waiting for transfers between devices, from_everyone(): return lax.all_to_all(copies, axis, split_axis=0, concat_axis=0, tiled=True)  34.5 us
    all_to_all x2, starting transfers between devices, send_sectioned(): lax.all_to_all(slot_block, 'expert', split_axis=1, concat_axis=0, tiled=T...  30.7 us
    all_to_all x3, starting transfers between devices, from_everyone(): return lax.all_to_all(copies, axis, split_axis=0, concat_axis=0, tiled=True)  21.1 us
    all_to_all x2, waiting for transfers between devices, sum_sectioned(): lax.all_to_all(summed.astype(jnp.bfloat16), 'expert', split_axis=0, conca...  20.6 us
    all_to_all x2, waiting for transfers between devices, send_sectioned(): lax.all_to_all(slot_block, 'expert', split_axis=1, concat_axis=0, tiled=T...  19 us
    all_to_all x1, waiting for transfers between devices, summed_rows(): return jnp.sum(lax.all_to_all(own, far, 0, 0, tiled=True), axis=0)  13.5 us
    all_to_all x2, starting transfers between devices, sum_sectioned(): lax.all_to_all(summed.astype(jnp.bfloat16), 'expert', split_axis=0, conca...  9.76 us
  transfers between devices with their start and end apart: 10, of which 10 were waited for; matrix products, arithmetic and copies ran while one was open for 11% of the time, Pallas kernels for 0%

commit v1 on v0

v1 whole, which is shorter than its diff:
```python
import functools
import types

import jax
import jax.numpy as jnp
from jax import lax
from jax.experimental import pallas as pl
from jax.experimental.pallas import tpu as pltpu
from jax.sharding import PartitionSpec as P

MESH = pl.DeviceIdType.MESH
BF16 = jnp.bfloat16
F32 = jnp.float32
LANES = 128
ROOT_HALF = 0.7071067811865476
ROOT_TAU = 0.3989422804014327
SPAN = 4

NT = (((1,), (1,)), ((), ()))
NN = (((1,), (0,)), ((), ()))


def dot(a, b, dims=NN):
    return lax.dot_general(a, b, dims, preferred_element_type=F32)


def gelu_exact(value):
    return 0.5 * value * (1.0 + lax.erf(value * ROOT_HALF))


def gelu_slope(value):
    return 0.5 * (1.0 + lax.erf(value * ROOT_HALF)) + value * jnp.exp(-0.5 * value * value) * ROOT_TAU


def scratch_plan(E, H, J, T, TP, S, D, FF):
    X, C = H // 2, D // LANES
    msg = J * C
    vm, dma = pltpu.VMEM, pltpu.SemaphoreType.DMA
    return dict(
        tok=vm((TP, D), BF16),
        cot=vm((TP, D), BF16),
        up=vm((J, D, FF), BF16),
        down=vm((J, FF, D), BF16),
        stage=vm((S * C, LANES), F32),
        a_send=vm((2, E, msg, LANES), BF16),
        a_recv=vm((2, E, msg, LANES), BF16),
        g=vm((2, J, H, E, D), BF16),
        pre=vm((J, H * E, FF), F32),
        part=vm((2, J, H, E, D), F32),
        d_send=vm((2, X, 2, J // 2, E, D), BF16),
        d_recv=vm((2, X, 2, J // 2, E, D), BF16),
        r1_send=vm((2, 2, J // 2, E, D), BF16),
        r1_recv=vm((2, 2, J // 2, E, D), BF16),
        r2_send=vm((2, 2, 2, J // 2, E, D), BF16),
        r2_recv=vm((2, 2, 2, J // 2, E, D), BF16),
        b_send=vm((2, E, msg, LANES), BF16),
        b_recv=vm((2, E, msg, LANES), BF16),
        slots=vm((2, S, D), BF16),
        comb=vm((TP, S), F32),
        comb_t=vm((S, TP), F32),
        disp=vm((TP, S), F32),
        disp_t=vm((S, TP), F32),
        grad_c=vm((TP, S), BF16),
        dsp_c=vm((S, D), F32),
        c_send=vm((H, S, LANES), BF16),
        c_own=vm((H, S, LANES), F32),
        c_recv=vm((H, S, LANES), BF16),
        n_all=vm((SPAN, S, LANES), BF16),
        n_send=vm((S, LANES), BF16),
        w_all=vm((E // SPAN, S, LANES), BF16),
        w_send=vm((S, LANES), BF16),
        f_all=vm((H, S, LANES), BF16),
        f_send=vm((S, LANES), BF16),
        in_sem=dma((2,)),
        a_ss=dma((2,)),
        a_rs=dma((2,)),
        g_ss=dma((2,)),
        g_rs=dma((2, 7)),
        d_ss=dma((2,)),
        d_rs=dma((2, X, 2)),
        r1_ss=dma((2,)),
        r1_rs=dma((2, 2)),
        r2_ss=dma((2,)),
        r2_rs=dma((2,)),
        b_ss=dma((2,)),
        b_rs=dma((2,)),
        c_ss=dma((4,)),
        c_rs=dma((4,)),
    )


def step_kernel(size, names, tok_in, sp, up_hbm, down_hbm, cot_in, mixed_out, dtok_out, dsp_out, *scratch):
    E, H, J, T, TP, S, D, FF = size
    X, C = H // 2, D // LANES
    half = J // 2
    v = types.SimpleNamespace(**dict(zip(names, scratch, strict=True)))
    ex = lax.axis_index("expert")
    hi = lax.axis_index("hidden")
    x, core = lax.div(hi, 2), lax.rem(hi, 2)

    def chip(dx):
        return lax.rem(x + dx + X, X)

    def at(dx, flip=0):
        return chip(dx) * 2 + (1 - core if flip else core)

    def copy(src, dst, ss, rs, e=None, h=None):
        return pltpu.make_async_remote_copy(
            src_ref=src,
            dst_ref=dst,
            send_sem=ss,
            recv_sem=rs,
            device_id={"expert": ex if e is None else e, "hidden": hi if h is None else h},
            device_id_type=MESH,
        )

    loads = [
        pltpu.make_async_copy(src, dst, v.in_sem.at[i])
        for i, (src, dst) in enumerate([(up_hbm, v.up), (down_hbm, v.down)])
    ]
    for load in loads:
        load.start()

    barrier = pltpu.get_barrier_semaphore()

    def greet_z(i, carry):
        pl.semaphore_signal(
            barrier, inc=1, device_id={"expert": lax.rem(ex + i, E), "hidden": hi}, device_id_type=MESH
        )
        return carry

    def greet_x(i, carry):
        pl.semaphore_signal(
            barrier, inc=1, device_id={"expert": ex, "hidden": lax.rem(hi + i, H)}, device_id_type=MESH
        )
        return carry

    lax.fori_loop(1, E, greet_z, 0)
    lax.fori_loop(1, H, greet_x, 0)

    def far_first(i):
        return E // 2 + (1 - 2 * lax.rem(i, 2)) * lax.div(i + 1, 2)

    def z_start(send, recv, ss, rs):
        def body(i, carry):
            peer = lax.rem(ex + far_first(i), E)
            copy(send.at[peer], recv.at[ex], ss, rs, e=peer).start()
            return carry

        lax.fori_loop(0, E - 1, body, 0)
        recv[ex] = send[ex]

    def landed(ref, sem):
        copy(ref, ref, sem, sem, h=at(0, 1)).wait_recv()

    def left(ref, sem):
        copy(ref, ref, sem, sem, h=at(0, 1)).wait_send()

    stage = v.stage

    def dispatch(k, value):
        for c in range(C):
            stage[c * S : (c + 1) * S, :] = value[:, c * LANES : (c + 1) * LANES]
        for e in range(E):
            rows = [stage[pl.ds(e * J + j, C, stride=S), :] for j in range(J)]
            v.a_send[k, e] = jnp.concatenate(rows, axis=0).astype(BF16)
        z_start(v.a_send.at[k], v.a_recv.at[k], v.a_ss.at[k], v.a_rs.at[k])

    lo, up = pl.ds(0, half), pl.ds(half, half)
    both = (lo, up)

    def pass_on(k, part, dx, to, sem):
        ref = v.g.at[k, both[part], at(dx)]
        copy(ref, ref, v.g_ss.at[k], v.g_rs.at[k, sem], h=to).start()

    def take(k, part, dx, sem):
        landed(v.g.at[k, both[part], at(dx)], v.g_rs.at[k, sem])
        pass_on(k, part, dx, at(0, 1), 6)

    def gather_start(k):
        landed(v.a_recv.at[k, pl.ds(0, E - 1)], v.a_rs.at[k])
        stage[...] = v.a_recv[k].reshape(E * J * C, LANES).astype(F32)
        for part in (0, 1):
            for j in range(part * half, (part + 1) * half):
                for c in range(C):
                    v.g[k, j, hi, :, c * LANES : (c + 1) * LANES] = stage[
                        pl.ds(j * C + c, E, stride=J * C), :
                    ].astype(BF16)
            pass_on(k, part, 0, at(1) if part == 0 else at(-1), 0 if part == 0 else 3)
        pass_on(k, 1, 0, at(1), 1)
        pass_on(k, 0, 0, at(-1), 2)
        for part in (0, 1):
            pass_on(k, part, 0, at(0, 1), 6)

    def gather_forward(k):
        take(k, 0, -1, 0)
        pass_on(k, 0, -1, at(1), 4)
        take(k, 1, 1, 3)
        pass_on(k, 1, 1, at(-1), 5)

    def gather_rest(k):
        take(k, 1, -1, 1)
        take(k, 0, 1, 2)

    def gather_far(k):
        take(k, 0, 2, 4)
        take(k, 1, 2, 5)

    def gather_finish(k):
        landed(v.g.at[k, :, pl.ds(0, X)], v.g_rs.at[k, 6])

    order = (2, 1, -1, 0)

    def d_copy(k, i, part):
        return copy(
            v.d_send.at[k, i, part], v.d_recv.at[k, i, part], v.d_ss.at[k], v.d_rs.at[k, i, part], h=at(0, 1)
        )

    def sum_start(k, part):
        for i, dx in enumerate(order):
            v.d_send[k, i, part] = v.part[k, both[part], at(dx, 1)].astype(BF16)
            d_copy(k, i, part).start()

    def chip_sum(k, i, part):
        return v.part[k, both[part], at(order[i])] + v.d_recv[k, i, part].astype(F32)

    def to_side(side):
        return at(1) if side == 0 else at(-1)

    def r2_send(k, side, part, value):
        v.r2_send[k, side, part] = value.astype(BF16)
        copy(
            v.r2_send.at[k, side, part], v.r2_recv.at[k, side, part], v.r2_ss.at[k], v.r2_rs.at[k], h=to_side(side)
        ).start()

    def sum_middle(k, part):
        d_copy(k, 0, part).wait_recv()
        v.r1_send[k, part] = chip_sum(k, 0, part).astype(BF16)
        copy(
            v.r1_send.at[k, part], v.r1_recv.at[k, part], v.r1_ss.at[k], v.r1_rs.at[k, part], h=to_side(part)
        ).start()
        near = 2 - part
        d_copy(k, near, part).wait_recv()
        r2_send(k, 1 - part, part, chip_sum(k, near, part))

    def sum_last(k, part):
        landed(v.r1_recv.at[k, part], v.r1_rs.at[k, part])
        near = 1 + part
        d_copy(k, near, part).wait_recv()
        r2_send(k, part, part, chip_sum(k, near, part) + v.r1_recv[k, part].astype(F32))

    def sum_return(k):
        for part in (0, 1):
            d_copy(k, 3, part).wait_recv()
        landed(v.r2_recv.at[k], v.r2_rs.at[k])
        for j in range(J):
            part, inner = divmod(j, half)
            total = v.part[k, j, at(0)] + v.d_recv[k, 3, part, inner].astype(F32)
            total = total + v.r2_recv[k, 0, part, inner].astype(F32) + v.r2_recv[k, 1, part, inner].astype(F32)
            for c in range(C):
                stage[pl.ds(j * C + c, E, stride=J * C), :] = total[:, c * LANES : (c + 1) * LANES]
        v.b_send[k] = stage[...].astype(BF16).reshape(E, J * C, LANES)
        z_start(v.b_send.at[k], v.b_recv.at[k], v.b_ss.at[k], v.b_rs.at[k])

    def collect(k):
        landed(v.b_recv.at[k, pl.ds(0, E - 1)], v.b_rs.at[k])
        stage[...] = v.b_recv[k].reshape(E * J * C, LANES).astype(F32)
        for c in range(C):
            v.slots[k, :, c * LANES : (c + 1) * LANES] = stage[pl.ds(c, S, stride=C), :].astype(BF16)

    tail = T - T % 16
    v.tok[tail:, :] = jnp.zeros((TP - tail, D), BF16)
    v.tok[:T, :] = tok_in[...]
    logits_t = dot(sp[...], v.tok[...], NT)
    held = lax.broadcasted_iota(jnp.int32, (S, TP), 1) < T
    masked = jnp.where(held, logits_t, -jnp.inf)
    raised = jnp.exp(masked - jnp.max(masked, axis=1, keepdims=True))
    disp_t = raised / jnp.sum(raised, axis=1, keepdims=True)
    v.disp_t[...] = disp_t
    slots_in = dot(disp_t.astype(BF16), v.tok[...])
    pl.semaphore_wait(barrier, E - 1 + H - 1)
    dispatch(0, slots_in)

    raised = jnp.exp(logits_t - jnp.max(logits_t, axis=0, keepdims=True))
    comb_t = raised / jnp.sum(raised, axis=0, keepdims=True)
    v.comb_t[...] = comb_t
    v.cot[tail:, :] = jnp.zeros((TP - tail, D), BF16)
    v.cot[:T, :] = cot_in[...]
    dispatch(1, dot(comb_t.astype(BF16), v.cot[...]))

    logits = dot(v.tok[...], sp[...], NT)
    held = lax.broadcasted_iota(jnp.int32, (TP, S), 0) < T
    masked = jnp.where(held, logits, -jnp.inf)
    raised = jnp.exp(masked - jnp.max(masked, axis=0, keepdims=True))
    v.disp[...] = raised / jnp.sum(raised, axis=0, keepdims=True)
    raised = jnp.exp(logits - jnp.max(logits, axis=1, keepdims=True))
    v.comb[...] = raised / jnp.sum(raised, axis=1, keepdims=True)

    def forward(j, carry):
        pre = dot(v.g[0, j].reshape(H * E, D), v.up[j])
        v.pre[j] = pre
        out = dot(gelu_exact(pre).astype(BF16), v.down[j])
        v.part[0, j] = out.reshape(H, E, D)
        return carry

    def slopes(j, carry):
        v.pre[j] = gelu_slope(v.pre[j])
        return carry

    def backward(j, carry):
        inward = dot(v.g[1, j].reshape(H * E, D), v.down[j], NT)
        d_pre = (inward * v.pre[j]).astype(BF16)
        v.part[1, j] = dot(d_pre, v.up[j], NT).reshape(H, E, D)
        return carry

    gather_start(0)
    gather_forward(0)
    gather_rest(0)
    gather_start(1)
    gather_far(0)
    gather_finish(0)
    for load in loads:
        load.wait()
    lax.fori_loop(0, half, forward, 0)
    gather_forward(1)
    sum_start(0, 0)
    lax.fori_loop(half, J, forward, 0)
    gather_rest(1)
    sum_start(0, 1)
    lax.fori_loop(0, J, slopes, 0)
    sum_middle(0, 0)
    sum_middle(0, 1)
    gather_far(1)
    gather_finish(1)
    lax.fori_loop(0, half, backward, 0)
    sum_start(1, 0)
    sum_last(0, 0)
    sum_last(0, 1)
    lax.fori_loop(half, J, backward, 0)
    sum_start(1, 1)
    sum_middle(1, 0)
    sum_middle(1, 1)
    sum_return(0)
    sum_last(1, 0)
    sum_last(1, 1)
    sum_return(1)

    collect(0)
    slots_out = v.slots[0]
    mixed = dot(v.comb[...].astype(BF16), slots_out)
    mixed_out[...] = mixed[:T].astype(BF16)
    comb_t = v.comb_t[...]
    d_comb = dot(slots_out, v.cot[...], NT)
    grad_ct = (comb_t * (d_comb - jnp.sum(comb_t * d_comb, axis=0, keepdims=True))).astype(BF16)
    v.dsp_c[...] = dot(grad_ct, v.tok[...])
    comb = v.comb[...]
    d_comb = dot(v.cot[...], slots_out, NT)
    v.grad_c[...] = (comb * (d_comb - jnp.sum(comb * d_comb, axis=1, keepdims=True))).astype(BF16)

    collect(1)
    d_slots = v.slots[1]
    disp_t = v.disp_t[...]
    d_disp = dot(d_slots, v.tok[...], NT)
    grad_dt = (disp_t * (d_disp - jnp.sum(disp_t * d_disp, axis=1, keepdims=True))).astype(BF16)
    grad = dot(grad_dt, v.tok[...]) + v.dsp_c[...]
    for h in range(H):
        block = grad[:, h * LANES : (h + 1) * LANES]
        v.c_own[h] = block
        v.c_send[h] = block.astype(BF16)

    def c_copy(slot):
        dx, flip = divmod(slot, 2)
        peer = at(dx, flip)
        return copy(v.c_send.at[peer], v.c_recv.at[slot], v.c_ss.at[0], v.c_rs.at[0], h=peer)

    row = (4, 5, 2, 3, 6, 7, 1)
    for slot in row:
        c_copy(slot).start()

    d_disp = dot(v.tok[...], d_slots, NT)
    disp = v.disp[...]
    grad_d = (disp * (d_disp - jnp.sum(disp * d_disp, axis=0, keepdims=True))).astype(BF16)
    d_tok = dot(disp.astype(BF16), d_slots) + dot(v.grad_c[...], sp[...]) + dot(grad_d, sp[...])
    dtok_out[...] = d_tok[:T].astype(BF16)

    total = v.c_own[hi]
    landed(v.c_recv.at[pl.ds(0, H - 1)], v.c_rs.at[0])
    for slot in row:
        total = total + v.c_recv[slot].astype(F32)

    place, base = lax.rem(ex, SPAN), lax.div(ex, SPAN)
    groups = E // SPAN
    near = total.astype(BF16)
    v.n_send[...] = near
    v.n_all[place] = near

    def n_copy(off):
        peer = base * SPAN + lax.rem(place + off, SPAN)
        return copy(v.n_send, v.n_all.at[place], v.c_ss.at[1], v.c_rs.at[1], e=peer)

    for off in range(1, SPAN):
        n_copy(off).start()
    landed(v.n_all.at[pl.ds(0, SPAN - 1)], v.c_rs.at[1])
    total = v.n_all[0].astype(F32)
    for i in range(1, SPAN):
        total = total + v.n_all[i].astype(F32)
    near = total.astype(BF16)
    v.w_send[...] = near
    v.w_all[base] = near

    def w_copy(off):
        peer = lax.rem(base + off, groups) * SPAN + place
        return copy(v.w_send, v.w_all.at[base], v.c_ss.at[2], v.c_rs.at[2], e=peer)

    far = sorted(range(1, groups), key=lambda off: -min(off, groups - off))
    for off in far:
        w_copy(off).start()
    landed(v.w_all.at[pl.ds(0, groups - 1)], v.c_rs.at[2])
    total = v.w_all[0].astype(F32)
    for i in range(1, groups):
        total = total + v.w_all[i].astype(F32)
    near = total.astype(BF16)
    v.f_send[...] = near
    v.f_all[hi] = near

    def f_copy(slot):
        dx, flip = divmod(slot, 2)
        return copy(v.f_send, v.f_all.at[hi], v.c_ss.at[3], v.c_rs.at[3], h=at(dx, flip))

    for slot in row:
        f_copy(slot).start()
    landed(v.f_all.at[pl.ds(0, H - 1)], v.c_rs.at[3])
    for h in range(H):
        dsp_out[:, h * LANES : (h + 1) * LANES] = v.f_all[h].astype(F32)

    for k in (0, 1):
        left(v.a_send.at[k, pl.ds(0, E - 1)], v.a_ss.at[k])
        left(v.b_send.at[k, pl.ds(0, E - 1)], v.b_ss.at[k])
        left(v.g.at[k, :, pl.ds(0, H - 1)], v.g_ss.at[k])
        left(v.d_send.at[k], v.d_ss.at[k])
        left(v.r1_send.at[k], v.r1_ss.at[k])
        left(v.r2_send.at[k], v.r2_ss.at[k])
    left(v.c_send.at[pl.ds(0, H - 1)], v.c_ss.at[0])
    left(v.n_all.at[pl.ds(0, SPAN - 1)], v.c_ss.at[1])
    left(v.w_all.at[pl.ds(0, groups - 1)], v.c_ss.at[2])
    left(v.f_all.at[pl.ds(0, H - 1)], v.c_ss.at[3])


def per_device(E, H, tokens, slot_params, expert_up, expert_down, cotangent):
    images, T, D = tokens.shape
    S = slot_params.shape[1]
    J, _, FF = expert_up.shape
    assert images == 1 and S == E * J and H == 8 and E % SPAN == 0 and D == H * LANES and J % 2 == 0
    size = (E, H, J, T, -(-T // LANES) * LANES, S, D, FF)
    plan = scratch_plan(*size)
    anywhere, local = pl.BlockSpec(memory_space=pl.ANY), pl.BlockSpec(memory_space=pltpu.VMEM)
    mixed, d_tokens, d_params = pl.pallas_call(
        functools.partial(step_kernel, size, tuple(plan)),
        out_shape=(
            jax.ShapeDtypeStruct((T, D), BF16),
            jax.ShapeDtypeStruct((T, D), BF16),
            jax.ShapeDtypeStruct((S, D), F32),
        ),
        in_specs=[local, local, anywhere, anywhere, local],
        out_specs=(local,) * 3,
        scratch_shapes=list(plan.values()),
        compiler_params=pltpu.CompilerParams(
            collective_id=0, has_side_effects=True, vmem_limit_bytes=52 * 1024 * 1024
        ),
    )(tokens.reshape(T, D), slot_params.T, expert_up, expert_down, cotangent.reshape(T, D))
    return mixed[None], d_tokens[None], d_params.T


def solution(mesh):
    own = P(("groups", "expert", "hidden"), None, None)
    return jax.shard_map(
        functools.partial(per_device, mesh.shape["expert"], mesh.shape["hidden"]),
        mesh=mesh,
        in_specs=(
            own,
            P("groups", None),
            P(("groups", "expert"), None, "hidden"),
            P(("groups", "expert"), "hidden", None),
            own,
        ),
        out_specs=(own, own, P("groups", None)),
        check_vma=False,
    )
```

time: 271 us -> 98.7 us (0.36)
  waiting for transfers between devices: 126 us -> 0 us
  Pallas kernels: 0 us -> 92.8 us
  starting transfers between devices: 77.7 us -> 0 us
  matrix products: 18.4 us -> 0 us
  local copies, waits for them, and re-layouts: 22.1 us -> 5.11 us
  blocking collectives: 14.7 us -> 0 us
  other arithmetic: 9.97 us -> 0 us
    all_to_all x10 -> x0, waiting for transfers between devices: 126 us -> none  [the longest x2 38.3 us: summed_on_arrival(): lax.all_to_all(blocks, axis, split_axis=0, concat_axis=0, tiled=True)]
    pallas_call x0 -> x1, Pallas kernels: none -> 92.8 us  [per_device(): pl.pallas_call(functools.partial(step_kernel, size, tuple(plan)), out_sha...]
    all_to_all x10 -> x0, starting transfers between devices: 77.7 us -> none  [the longest x2 30.7 us: send_sectioned(): lax.all_to_all(slot_block, 'expert', split_axis=1, concat_axis=0, tiled=T...]
    dot_general x14 -> x0, matrix products: 18.4 us -> none  [the longest x1 8 us: back_in(): jnp.einsum('iesf,edf->iesd', dpre_block, expert_up, preferred_element_typ...]
    all_to_all x2 -> x0, blocking collectives: 14.7 us -> none  [the longest x1 7.58 us: summed_on_arrival(): lax.all_to_all(blocks, axis, split_axis=0, concat_axis=0, tiled=True)]
    all_to_all x4 -> x0, other arithmetic: 4.96 us -> none  [the longest x2 2.48 us: from_everyone(): return lax.all_to_all(copies, axis, split_axis=0, concat_axis=0, tiled=True)]
    another operation x4 -> x0, local copies, waits for them, and re-layouts: 4.69 us -> none  [the longest x2 4.62 us: in_blocks(): x.reshape(*dims[:dim], devices, dims[dim] // devices, *dims[dim + 1:])]
    all_to_all x9 -> x0, local copies, waits for them, and re-layouts: 4.65 us -> none  [the longest x2 2.41 us: from_everyone(): return lax.all_to_all(copies, axis, split_axis=0, concat_axis=0, tiled=True)]
  transfers between devices with their start and end apart: 10 -> 0, of which waited for: 10 -> 0; matrix products, arithmetic and copies ran while one was open for 11% -> 0% of each run, Pallas kernels for 0% -> 0%
where the time goes in v1:
time: 98.7 us; the launch traced here: 98.5 us
  Pallas kernels  92.8 us (94%)
  local copies, waits for them, and re-layouts  5.11 us (5%)
    pallas_call x1, Pallas kernels, per_device(): pl.pallas_call(functools.partial(step_kernel, size, tuple(plan)), out_sha...  92.8 us
    unnamed x9, local copies, waits for them, and re-layouts  5.11 us

profile of v1, /device:TPU:33, one launch (start us, length us, event | category | flops | bytes accessed | tf_op | source)
XLA Modules:
  0.0 98.5 jit_solution(12488485094826658972)
XLA Ops:
  0.6 0.0 copy-start
  0.6 1.0 %copy-done = bf16[1,196,1024]{2,1,0:T(8,128)(2,1)S(1)} copy-done((bf16[1,196,1024]{2,1,0:T(8,128)(2,1)S(1)}, bf16[1,196,1024]{2,1,0:T(8,128)(2,1)}, u32[]{:S(2)}) %copy-start) | copy-done | bytes 401432
  1.6 0.0 copy-start.1
  1.6 1.0 %copy-done.1 = bf16[1,196,1024]{2,1,0:T(8,128)(2,1)S(1)} copy-done((bf16[1,196,1024]{2,1,0:T(8,128)(2,1)S(1)}, bf16[1,196,1024]{2,1,0:T(8,128)(2,1)}, u32[]{:S(2)}) %copy-start.1) | copy-done | bytes 401432
  2.6 0.0 copy-start.2
  2.6 0.9 copy-done.2
  3.5 92.8 %shard_map.76 = (bf16[196,1024]{1,0:T(8,128)(2,1)S(1)}, bf16[196,1024]{1,0:T(8,128)(2,1)S(1)}, f32[64,1024]{1,0:T(8,128)S(1)}) custom-call(bf16[196,1024]{1,0:T(8,128)(2,1)S(1)} %bitcast.8, bf16[64,1024]{1,0:T(8,128)(2,1)S(1)} %bitcast.11, bf16[4,1024,512]{2,1,0:T(8,128)(2,1)} %up_hbm.1, bf16[4,512,1024]{2,1,0:T(8,128)(2,1)} %down_hbm.1, ...), custom_call_target="tpu_custom_call" | custom-call | tf_op jit(solution)/shard_map/pallas_call | solution.py:457
  96.3 0.8 copy.11
  97.1 0.8 copy.12
  97.8 0.7 copy.13
Async XLA Ops:
  0.6 1.0 %copy-start = (bf16[1,196,1024]{2,1,0:T(8,128)(2,1)S(1)}, bf16[1,196,1024]{2,1,0:T(8,128)(2,1)}, u32[]{:S(2)}) copy-start(bf16[1,196,1024]{2,1,0:T(8,128)(2,1)} %param.5) | copy-start | bytes 1204228
  1.6 1.0 %copy-start.1 = (bf16[1,196,1024]{2,1,0:T(8,128)(2,1)S(1)}, bf16[1,196,1024]{2,1,0:T(8,128)(2,1)}, u32[]{:S(2)}) copy-start(bf16[1,196,1024]{2,1,0:T(8,128)(2,1)} %param.9) | copy-start | bytes 1204228
  2.6 0.9 copy-start.2

commit v2 on v1

--- a/solution.py
+++ b/solution.py
@@ -37,24 +37,28 @@
     msg = J * C
     vm, dma = pltpu.VMEM, pltpu.SemaphoreType.DMA
     return dict(
+        tok_in=vm((T, D), BF16),
+        cot_in=vm((T, D), BF16),
         tok=vm((TP, D), BF16),
         cot=vm((TP, D), BF16),
         up=vm((J, D, FF), BF16),
         down=vm((J, FF, D), BF16),
+        up_t=vm((J, FF, D), BF16),
+        down_t=vm((J, D, FF), BF16),
         stage=vm((S * C, LANES), F32),
         a_send=vm((2, E, msg, LANES), BF16),
         a_recv=vm((2, E, msg, LANES), BF16),
         g=vm((2, J, H, E, D), BF16),
         pre=vm((J, H * E, FF), F32),
         part=vm((2, J, H, E, D), F32),
-        d_send=vm((2, X, 2, J // 2, E, D), BF16),
-        d_recv=vm((2, X, 2, J // 2, E, D), BF16),
-        r1_send=vm((2, 2, J // 2, E, D), BF16),
-        r1_recv=vm((2, 2, J // 2, E, D), BF16),
-        r2_send=vm((2, 2, 2, J // 2, E, D), BF16),
-        r2_recv=vm((2, 2, 2, J // 2, E, D), BF16),
-        b_send=vm((2, E, msg, LANES), BF16),
-        b_recv=vm((2, E, msg, LANES), BF16),
+        d_send=vm((2, X, J, E, D), BF16),
+        d_recv=vm((2, X, J, E, D), BF16),
+        r1_send=vm((2, J, E, D), BF16),
+        r1_recv=vm((2, J, E, D), BF16),
+        r2_send=vm((2, 2, J, E, D), BF16),
+        r2_recv=vm((2, 2, J, E, D), BF16),
+        b_send=vm((2, 2, E, msg // 2, LANES), BF16),
+        b_recv=vm((2, 2, E, msg // 2, LANES), BF16),
         slots=vm((2, S, D), BF16),
         comb=vm((TP, S), F32),
         comb_t=vm((S, TP), F32),
@@ -71,25 +75,25 @@
         w_send=vm((S, LANES), BF16),
         f_all=vm((H, S, LANES), BF16),
         f_send=vm((S, LANES), BF16),
-        in_sem=dma((2,)),
+        in_sem=dma((4,)),
         a_ss=dma((2,)),
         a_rs=dma((2,)),
         g_ss=dma((2,)),
         g_rs=dma((2, 7)),
         d_ss=dma((2,)),
-        d_rs=dma((2, X, 2)),
+        d_rs=dma((2, X, J)),
         r1_ss=dma((2,)),
-        r1_rs=dma((2, 2)),
+        r1_rs=dma((2, J)),
         r2_ss=dma((2,)),
-        r2_rs=dma((2,)),
-        b_ss=dma((2,)),
-        b_rs=dma((2,)),
+        r2_rs=dma((2, 2)),
+        b_ss=dma((2, 2)),
+        b_rs=dma((2, 2)),
         c_ss=dma((4,)),
         c_rs=dma((4,)),
     )
 
 
-def step_kernel(size, names, tok_in, sp, up_hbm, down_hbm, cot_in, mixed_out, dtok_out, dsp_out, *scratch):
+def step_kernel(size, names, tok_hbm, sp, up_hbm, down_hbm, cot_hbm, mixed_out, dtok_out, dsp_out, *scratch):
     E, H, J, T, TP, S, D, FF = size
     X, C = H // 2, D // LANES
     half = J // 2
@@ -114,10 +118,8 @@
             device_id_type=MESH,
         )
 
-    loads = [
-        pltpu.make_async_copy(src, dst, v.in_sem.at[i])
-        for i, (src, dst) in enumerate([(up_hbm, v.up), (down_hbm, v.down)])
-    ]
+    pairs = [(tok_hbm, v.tok_in), (cot_hbm, v.cot_in), (up_hbm, v.up), (down_hbm, v.down)]
+    loads = [pltpu.make_async_copy(src, dst, v.in_sem.at[i]) for i, (src, dst) in enumerate(pairs)]
     for load in loads:
         load.start()
 
@@ -211,66 +213,63 @@
 
     order = (2, 1, -1, 0)
 
-    def d_copy(k, i, part):
-        return copy(
-            v.d_send.at[k, i, part], v.d_recv.at[k, i, part], v.d_ss.at[k], v.d_rs.at[k, i, part], h=at(0, 1)
-        )
-
-    def sum_start(k, part):
+    def d_copy(k, i, j):
+        return copy(v.d_send.at[k, i, j], v.d_recv.at[k, i, j], v.d_ss.at[k], v.d_rs.at[k, i, j], h=at(0, 1))
+
+    def sum_start(k, j):
         for i, dx in enumerate(order):
-            v.d_send[k, i, part] = v.part[k, both[part], at(dx, 1)].astype(BF16)
-            d_copy(k, i, part).start()
-
-    def chip_sum(k, i, part):
-        return v.part[k, both[part], at(order[i])] + v.d_recv[k, i, part].astype(F32)
+            v.d_send[k, i, j] = v.part[k, j, at(dx, 1)].astype(BF16)
+            d_copy(k, i, j).start()
+
+    def chip_sum(k, i, j):
+        d_copy(k, i, j).wait_recv()
+        return v.part[k, j, at(order[i])] + v.d_recv[k, i, j].astype(F32)
 
     def to_side(side):
         return at(1) if side == 0 else at(-1)
 
-    def r2_send(k, side, part, value):
-        v.r2_send[k, side, part] = value.astype(BF16)
+    def r2_send(k, side, j, value):
+        v.r2_send[k, side, j] = value.astype(BF16)
         copy(
-            v.r2_send.at[k, side, part], v.r2_recv.at[k, side, part], v.r2_ss.at[k], v.r2_rs.at[k], h=to_side(side)
+            v.r2_send.at[k, side, j], v.r2_recv.at[k, side, j], v.r2_ss.at[k], v.r2_rs.at[k, j // half], h=to_side(side)
         ).start()
 
-    def sum_middle(k, part):
-        d_copy(k, 0, part).wait_recv()
-        v.r1_send[k, part] = chip_sum(k, 0, part).astype(BF16)
-        copy(
-            v.r1_send.at[k, part], v.r1_recv.at[k, part], v.r1_ss.at[k], v.r1_rs.at[k, part], h=to_side(part)
-        ).start()
-        near = 2 - part
-        d_copy(k, near, part).wait_recv()
-        r2_send(k, 1 - part, part, chip_sum(k, near, part))
-
-    def sum_last(k, part):
-        landed(v.r1_recv.at[k, part], v.r1_rs.at[k, part])
-        near = 1 + part
-        d_copy(k, near, part).wait_recv()
-        r2_send(k, part, part, chip_sum(k, near, part) + v.r1_recv[k, part].astype(F32))
-
-    def sum_return(k):
+    def sum_middle(k, j):
+        part = j // half
+        v.r1_send[k, j] = chip_sum(k, 0, j).astype(BF16)
+        copy(v.r1_send.at[k, j], v.r1_recv.at[k, j], v.r1_ss.at[k], v.r1_rs.at[k, j], h=to_side(part)).start()
+        r2_send(k, 1 - part, j, chip_sum(k, 2 - part, j))
+
+    def sum_last(k, j):
+        part = j // half
+        landed(v.r1_recv.at[k, j], v.r1_rs.at[k, j])
+        r2_send(k, part, j, chip_sum(k, 1 + part, j) + v.r1_recv[k, j].astype(F32))
+
+    def sum_return(k, part):
+        landed(v.r2_recv.at[k, 0], v.r2_rs.at[k, part])
+        rows = half * C
+        for inner in range(half):
+            j = part * half + inner
+            total = chip_sum(k, 3, j) + v.r2_recv[k, 0, j].astype(F32) + v.r2_recv[k, 1, j].astype(F32)
+            for c in range(C):
+                stage[pl.ds(inner * C + c, E, stride=rows), :] = total[:, c * LANES : (c + 1) * LANES]
+        v.b_send[k, part] = stage[: E * rows, :].astype(BF16).reshape(E, rows, LANES)
+        z_start(v.b_send.at[k, part], v.b_recv.at[k, part], v.b_ss.at[k, part], v.b_rs.at[k, part])
+
+    def collect(k):
+        rows = half * C
         for part in (0, 1):
-            d_copy(k, 3, part).wait_recv()
-        landed(v.r2_recv.at[k], v.r2_rs.at[k])
-        for j in range(J):
-            part, inner = divmod(j, half)
-            total = v.part[k, j, at(0)] + v.d_recv[k, 3, part, inner].astype(F32)
-            total = total + v.r2_recv[k, 0, part, inner].astype(F32) + v.r2_recv[k, 1, part, inner].astype(F32)
-            for c in range(C):
-                stage[pl.ds(j * C + c, E, stride=J * C), :] = total[:, c * LANES : (c + 1) * LANES]
-        v.b_send[k] = stage[...].astype(BF16).reshape(E, J * C, LANES)
-        z_start(v.b_send.at[k], v.b_recv.at[k], v.b_ss.at[k], v.b_rs.at[k])
-
-    def collect(k):
-        landed(v.b_recv.at[k, pl.ds(0, E - 1)], v.b_rs.at[k])
-        stage[...] = v.b_recv[k].reshape(E * J * C, LANES).astype(F32)
+            landed(v.b_recv.at[k, part, pl.ds(0, E - 1)], v.b_rs.at[k, part])
+            for e in range(E):
+                at_row = (2 * e + part) * rows
+                stage[at_row : at_row + rows, :] = v.b_recv[k, part, e].astype(F32)
         for c in range(C):
             v.slots[k, :, c * LANES : (c + 1) * LANES] = stage[pl.ds(c, S, stride=C), :].astype(BF16)
 
+    loads[0].wait()
     tail = T - T % 16
     v.tok[tail:, :] = jnp.zeros((TP - tail, D), BF16)
-    v.tok[:T, :] = tok_in[...]
+    v.tok[:T, :] = v.tok_in[...]
     logits_t = dot(sp[...], v.tok[...], NT)
     held = lax.broadcasted_iota(jnp.int32, (S, TP), 1) < T
     masked = jnp.where(held, logits_t, -jnp.inf)
@@ -284,8 +283,9 @@
     raised = jnp.exp(logits_t - jnp.max(logits_t, axis=0, keepdims=True))
     comb_t = raised / jnp.sum(raised, axis=0, keepdims=True)
     v.comb_t[...] = comb_t
+    loads[1].wait()
     v.cot[tail:, :] = jnp.zeros((TP - tail, D), BF16)
-    v.cot[:T, :] = cot_in[...]
+    v.cot[:T, :] = v.cot_in[...]
     dispatch(1, dot(comb_t.astype(BF16), v.cot[...]))
 
     logits = dot(v.tok[...], sp[...], NT)
@@ -296,54 +296,66 @@
     raised = jnp.exp(logits - jnp.max(logits, axis=1, keepdims=True))
     v.comb[...] = raised / jnp.sum(raised, axis=1, keepdims=True)
 
-    def forward(j, carry):
+    for load in loads[2:]:
+        load.wait()
+
+    def turn(j, carry):
+        v.up_t[j] = v.up[j].T
+        v.down_t[j] = v.down[j].T
+        return carry
+
+    lax.fori_loop(0, J, turn, 0)
+
+    def forward(j):
         pre = dot(v.g[0, j].reshape(H * E, D), v.up[j])
         v.pre[j] = pre
         out = dot(gelu_exact(pre).astype(BF16), v.down[j])
         v.part[0, j] = out.reshape(H, E, D)
-        return carry
 
     def slopes(j, carry):
         v.pre[j] = gelu_slope(v.pre[j])
         return carry
 
-    def backward(j, carry):
-        inward = dot(v.g[1, j].reshape(H * E, D), v.down[j], NT)
+    def backward(j):
+        inward = dot(v.g[1, j].reshape(H * E, D), v.down_t[j])
         d_pre = (inward * v.pre[j]).astype(BF16)
-        v.part[1, j] = dot(d_pre, v.up[j], NT).reshape(H, E, D)
-        return carry
-
+        v.part[1, j] = dot(d_pre, v.up_t[j]).reshape(H, E, D)
+
+    turns = [j + part * half for j in range(half) for part in (0, 1)]
     gather_start(0)
     gather_forward(0)
     gather_rest(0)
     gather_start(1)
     gather_far(0)
     gather_finish(0)
-    for load in loads:
-        load.wait()
-    lax.fori_loop(0, half, forward, 0)
-    gather_forward(1)
-    sum_start(0, 0)
-    lax.fori_loop(half, J, forward, 0)
+    for i, j in enumerate(turns):
+        forward(j)
+        sum_start(0, j)
+        if i == 1:
+            gather_forward(1)
+        if i > 0:
+            sum_middle(0, turns[i - 1])
     gather_rest(1)
-    sum_start(0, 1)
     lax.fori_loop(0, J, slopes, 0)
-    sum_middle(0, 0)
-    sum_middle(0, 1)
+    sum_middle(0, turns[-1])
     gather_far(1)
+    for j in turns[:2]:
+        sum_last(0, j)
     gather_finish(1)
-    lax.fori_loop(0, half, backward, 0)
-    sum_start(1, 0)
-    sum_last(0, 0)
-    sum_last(0, 1)
-    lax.fori_loop(half, J, backward, 0)
-    sum_start(1, 1)
-    sum_middle(1, 0)
-    sum_middle(1, 1)
-    sum_return(0)
-    sum_last(1, 0)
-    sum_last(1, 1)
-    sum_return(1)
+    for i, j in enumerate(turns):
+        backward(j)
+        sum_start(1, j)
+        if i > 0:
+            sum_middle(1, turns[i - 1])
+        if i < 2:
+            sum_last(0, turns[i + 2])
+    for part in (0, 1):
+        sum_return(0, part)
+    sum_middle(1, turns[-1])
+    for j in turns:
+        sum_last(1, j)
+    for part in (0, 1):
+        sum_return(1, part)
 
     collect(0)
     slots_out = v.slots[0]
@@ -409,7 +421,8 @@
     v.w_all[base] = near
 
     def w_copy(off):
-        peer = lax.rem(base + off, groups) * SPAN + place
+        side = lax.rem(place + SPAN // 2, SPAN) if 2 * off == groups else place
+        peer = lax.rem(base + off, groups) * SPAN + side
         return copy(v.w_send, v.w_all.at[base], v.c_ss.at[2], v.c_rs.at[2], e=peer)
 
     far = sorted(range(1, groups), key=lambda off: -min(off, groups - off))
@@ -435,7 +448,8 @@
 
     for k in (0, 1):
         left(v.a_send.at[k, pl.ds(0, E - 1)], v.a_ss.at[k])
-        left(v.b_send.at[k, pl.ds(0, E - 1)], v.b_ss.at[k])
+        for part in (0, 1):
+            left(v.b_send.at[k, part, pl.ds(0, E - 1)], v.b_ss.at[k, part])
         left(v.g.at[k, :, pl.ds(0, H - 1)], v.g_ss.at[k])
         left(v.d_send.at[k], v.d_ss.at[k])
         left(v.r1_send.at[k], v.r1_ss.at[k])
@@ -461,11 +475,11 @@
             jax.ShapeDtypeStruct((T, D), BF16),
             jax.ShapeDtypeStruct((S, D), F32),
         ),
-        in_specs=[local, local, anywhere, anywhere, local],
+        in_specs=[anywhere, local, anywhere, anywhere, anywhere],
         out_specs=(local,) * 3,
         scratch_shapes=list(plan.values()),
         compiler_params=pltpu.CompilerParams(
-            collective_id=0, has_side_effects=True, vmem_limit_bytes=52 * 1024 * 1024
+            collective_id=0, has_side_effects=True, vmem_limit_bytes=54016 * 1024
         ),
     )(tokens.reshape(T, D), slot_params.T, expert_up, expert_down, cotangent.reshape(T, D))
     return mixed[None], d_tokens[None], d_params.T

time: 98.7 us -> 95.8 us (0.971)
  local copies, waits for them, and re-layouts: 5.11 us -> 3.1 us
    unnamed x9 -> x5, local copies, waits for them, and re-layouts: 5.11 us -> 3.1 us
where the time goes in v2:
time: 95.8 us; the launch traced here: 95.6 us
  Pallas kernels  91.9 us (96%)
  local copies, waits for them, and re-layouts  3.1 us (3%)
    pallas_call x1, Pallas kernels, per_device(): pl.pallas_call(functools.partial(step_kernel, size, tuple(plan)), out_sha...  91.9 us
    unnamed x5, local copies, waits for them, and re-layouts  3.1 us

profile of v2, /device:TPU:33, one launch (start us, length us, event | category | flops | bytes accessed | tf_op | source)
XLA Modules:
  0.0 95.6 jit_solution(3688146976742494319)
XLA Ops:
  0.6 0.0 copy-start
  0.6 0.9 copy-done
  1.5 91.9 %shard_map.76 = (bf16[196,1024]{1,0:T(8,128)(2,1)S(1)}, bf16[196,1024]{1,0:T(8,128)(2,1)S(1)}, f32[64,1024]{1,0:T(8,128)S(1)}) custom-call(bf16[196,1024]{1,0:T(8,128)(2,1)} %bitcast.10, bf16[64,1024]{1,0:T(8,128)(2,1)S(1)} %bitcast.9, bf16[4,1024,512]{2,1,0:T(8,128)(2,1)} %up_hbm.1, bf16[4,512,1024]{2,1,0:T(8,128)(2,1)} %down_hbm.1, bf16[196,1024]{1,0:T(8,128)(2,1)} %bitcast.11), custom_call_target="tpu_custom_call" | custom-call | tf_op jit(solution)/shard_map/pallas_call | solution.py:471
  93.4 0.8 copy.11
  94.2 0.8 copy.12
  94.9 0.7 copy.13
Async XLA Ops:
  0.6 0.9 copy-start

commit v3 on v2

--- a/solution.py
+++ b/solution.py
@@ -160,12 +160,14 @@
 
     stage = v.stage
 
-    def dispatch(k, value):
+    def pack(k, value):
         for c in range(C):
             stage[c * S : (c + 1) * S, :] = value[:, c * LANES : (c + 1) * LANES]
         for e in range(E):
             rows = [stage[pl.ds(e * J + j, C, stride=S), :] for j in range(J)]
             v.a_send[k, e] = jnp.concatenate(rows, axis=0).astype(BF16)
+
+    def dispatch(k):
         z_start(v.a_send.at[k], v.a_recv.at[k], v.a_ss.at[k], v.a_rs.at[k])
 
     lo, up = pl.ds(0, half), pl.ds(half, half)
@@ -277,8 +279,7 @@
     disp_t = raised / jnp.sum(raised, axis=1, keepdims=True)
     v.disp_t[...] = disp_t
     slots_in = dot(disp_t.astype(BF16), v.tok[...])
-    pl.semaphore_wait(barrier, E - 1 + H - 1)
-    dispatch(0, slots_in)
+    pack(0, slots_in)
 
     raised = jnp.exp(logits_t - jnp.max(logits_t, axis=0, keepdims=True))
     comb_t = raised / jnp.sum(raised, axis=0, keepdims=True)
@@ -286,7 +287,10 @@
     loads[1].wait()
     v.cot[tail:, :] = jnp.zeros((TP - tail, D), BF16)
     v.cot[:T, :] = v.cot_in[...]
-    dispatch(1, dot(comb_t.astype(BF16), v.cot[...]))
+    pack(1, dot(comb_t.astype(BF16), v.cot[...]))
+    pl.semaphore_wait(barrier, E - 1 + H - 1)
+    dispatch(0)
+    dispatch(1)
 
     logits = dot(v.tok[...], sp[...], NT)
     held = lax.broadcasted_iota(jnp.int32, (TP, S), 0) < T
@@ -333,27 +337,28 @@
         sum_start(0, j)
         if i == 1:
             gather_forward(1)
+        if i == 2:
+            gather_rest(1)
         if i > 0:
             sum_middle(0, turns[i - 1])
-    gather_rest(1)
     lax.fori_loop(0, J, slopes, 0)
     sum_middle(0, turns[-1])
     gather_far(1)
-    for j in turns[:2]:
-        sum_last(0, j)
     gather_finish(1)
     for i, j in enumerate(turns):
         backward(j)
         sum_start(1, j)
         if i > 0:
             sum_middle(1, turns[i - 1])
-        if i < 2:
-            sum_last(0, turns[i + 2])
-    for part in (0, 1):
-        sum_return(0, part)
+        for one in turns[2 * i : 2 * i + 2]:
+            sum_last(0, one)
     sum_middle(1, turns[-1])
-    for j in turns:
-        sum_last(1, j)
+    sum_last(1, turns[0])
+    sum_return(0, 0)
+    sum_last(1, turns[1])
+    sum_last(1, turns[2])
+    sum_return(0, 1)
+    sum_last(1, turns[3])
     for part in (0, 1):
         sum_return(1, part)
 
@@ -460,6 +465,16 @@
     left(v.f_all.at[pl.ds(0, H - 1)], v.c_ss.at[3])
 
 
+def store_kernel(*refs):
+    count = len(refs) // 2
+    sems = refs[-1]
+    copies = [pltpu.make_async_copy(refs[i], refs[count + i], sems.at[i]) for i in range(count)]
+    for one in copies:
+        one.start()
+    for one in copies:
+        one.wait()
+
+
 def per_device(E, H, tokens, slot_params, expert_up, expert_down, cotangent):
     images, T, D = tokens.shape
     S = slot_params.shape[1]
@@ -468,13 +483,14 @@
     size = (E, H, J, T, -(-T // LANES) * LANES, S, D, FF)
     plan = scratch_plan(*size)
     anywhere, local = pl.BlockSpec(memory_space=pl.ANY), pl.BlockSpec(memory_space=pltpu.VMEM)
-    mixed, d_tokens, d_params = pl.pallas_call(
+    shapes = (
+        jax.ShapeDtypeStruct((T, D), BF16),
+        jax.ShapeDtypeStruct((T, D), BF16),
+        jax.ShapeDtypeStruct((S, D), F32),
+    )
+    results = pl.pallas_call(
         functools.partial(step_kernel, size, tuple(plan)),
-        out_shape=(
-            jax.ShapeDtypeStruct((T, D), BF16),
-            jax.ShapeDtypeStruct((T, D), BF16),
-            jax.ShapeDtypeStruct((S, D), F32),
-        ),
+        out_shape=shapes,
         in_specs=[anywhere, local, anywhere, anywhere, anywhere],
         out_specs=(local,) * 3,
         scratch_shapes=list(plan.values()),
@@ -482,6 +498,14 @@
             collective_id=0, has_side_effects=True, vmem_limit_bytes=54016 * 1024
         ),
     )(tokens.reshape(T, D), slot_params.T, expert_up, expert_down, cotangent.reshape(T, D))
+    mixed, d_tokens, d_params = pl.pallas_call(
+        store_kernel,
+        out_shape=shapes,
+        in_specs=[anywhere] * 3,
+        out_specs=(anywhere,) * 3,
+        scratch_shapes=[pltpu.SemaphoreType.DMA((3,))],
+        compiler_params=pltpu.CompilerParams(vmem_limit_bytes=1024 * 1024),
+    )(*results)
     return mixed[None], d_tokens[None], d_params.T
 
 

time: 95.8 us -> 95 us (level)
  local copies, waits for them, and re-layouts: 3.1 us -> 0.9 us
  Pallas kernels: 91.9 us -> 93.3 us
    unnamed x5 -> x2, local copies, waits for them, and re-layouts: 3.1 us -> 0.9 us
    pallas_call x0 -> x1, Pallas kernels: none -> 1 us  [per_device(): pl.pallas_call(store_kernel, out_shape=shapes, in_specs=[anywhere] * 3, o...]
where the time goes in v3:
time: 95 us; the launch traced here: 94.9 us
  Pallas kernels  93.3 us (98%)
    pallas_call x1, Pallas kernels, per_device(): pl.pallas_call(functools.partial(step_kernel, size, tuple(plan)), out_sha...  92.3 us

profile of v3, /device:TPU:33, one launch (start us, length us, event | category | flops | bytes accessed | tf_op | source)
XLA Modules:
  0.0 94.9 jit_solution(17039647224052588546)
XLA Ops:
  0.6 0.0 copy-start
  0.6 0.9 copy-done
  1.5 92.3 %shard_map.76 = (bf16[196,1024]{1,0:T(8,128)(2,1)S(1)}, bf16[196,1024]{1,0:T(8,128)(2,1)S(1)}, f32[64,1024]{1,0:T(8,128)S(1)}) custom-call(bf16[196,1024]{1,0:T(8,128)(2,1)} %bitcast.7, bf16[64,1024]{1,0:T(8,128)(2,1)S(1)} %bitcast.6, bf16[4,1024,512]{2,1,0:T(8,128)(2,1)} %up_hbm.1, bf16[4,512,1024]{2,1,0:T(8,128)(2,1)} %down_hbm.1, bf16[196,1024]{1,0:T(8,128)(2,1)} %bitcast.8), custom_call_target="tpu_custom_call" | custom-call | tf_op jit(solution)/shard_map/pallas_call | solution.py:491
  93.9 1.0 %shard_map.77 = (bf16[196,1024]{1,0:T(8,128)(2,1)}, bf16[196,1024]{1,0:T(8,128)(2,1)}, f32[64,1024]{1,0:T(8,128)}) custom-call(bf16[196,1024]{1,0:T(8,128)(2,1)S(1)} %get-tuple-element.9.refs_0_, bf16[196,1024]{1,0:T(8,128)(2,1)S(1)} %get-tuple-element.10.refs_1_, f32[64,1024]{1,0:T(8,128)S(1)} %get-tuple-element.11.refs_2_), custom_call_target="tpu_custom_call" | custom-call | tf_op jit(solution)/shard_map/pallas_call | solution.py:501
Async XLA Ops:
  0.6 0.9 copy-start

commit v4 on v3

--- a/solution.py
+++ b/solution.py
@@ -337,28 +337,27 @@
         sum_start(0, j)
         if i == 1:
             gather_forward(1)
-        if i == 2:
-            gather_rest(1)
         if i > 0:
             sum_middle(0, turns[i - 1])
+    gather_rest(1)
     lax.fori_loop(0, J, slopes, 0)
     sum_middle(0, turns[-1])
     gather_far(1)
+    for j in turns[:2]:
+        sum_last(0, j)
     gather_finish(1)
     for i, j in enumerate(turns):
         backward(j)
         sum_start(1, j)
         if i > 0:
             sum_middle(1, turns[i - 1])
-        for one in turns[2 * i : 2 * i + 2]:
-            sum_last(0, one)
+        if i < 2:
+            sum_last(0, turns[i + 2])
+    for part in (0, 1):
+        sum_return(0, part)
     sum_middle(1, turns[-1])
-    sum_last(1, turns[0])
-    sum_return(0, 0)
-    sum_last(1, turns[1])
-    sum_last(1, turns[2])
-    sum_return(0, 1)
-    sum_last(1, turns[3])
+    for j in turns:
+        sum_last(1, j)
     for part in (0, 1):
         sum_return(1, part)
 

time: 95 us -> 94.1 us (level)
  no operation moved by 1% of the time
where the time goes in v4:
time: 94.1 us; the launch traced here: 94 us
  Pallas kernels  92.5 us (98%)
    pallas_call x1, Pallas kernels, per_device(): pl.pallas_call(functools.partial(step_kernel, size, tuple(plan)), out_sha...  91.5 us

profile of v4, /device:TPU:33, one launch (start us, length us, event | category | flops | bytes accessed | tf_op | source)
XLA Modules:
  0.0 94.0 jit_solution(14286133710329559015)
XLA Ops:
  0.6 0.0 copy-start
  0.6 0.9 copy-done
  1.5 91.5 %shard_map.76 = (bf16[196,1024]{1,0:T(8,128)(2,1)S(1)}, bf16[196,1024]{1,0:T(8,128)(2,1)S(1)}, f32[64,1024]{1,0:T(8,128)S(1)}) custom-call(bf16[196,1024]{1,0:T(8,128)(2,1)} %bitcast.7, bf16[64,1024]{1,0:T(8,128)(2,1)S(1)} %bitcast.6, bf16[4,1024,512]{2,1,0:T(8,128)(2,1)} %up_hbm.1, bf16[4,512,1024]{2,1,0:T(8,128)(2,1)} %down_hbm.1, bf16[196,1024]{1,0:T(8,128)(2,1)} %bitcast.8), custom_call_target="tpu_custom_call" | custom-call | tf_op jit(solution)/shard_map/pallas_call | solution.py:490
  93.0 1.0 %shard_map.77 = (bf16[196,1024]{1,0:T(8,128)(2,1)}, bf16[196,1024]{1,0:T(8,128)(2,1)}, f32[64,1024]{1,0:T(8,128)}) custom-call(bf16[196,1024]{1,0:T(8,128)(2,1)S(1)} %get-tuple-element.9.refs_0_, bf16[196,1024]{1,0:T(8,128)(2,1)S(1)} %get-tuple-element.10.refs_1_, f32[64,1024]{1,0:T(8,128)S(1)} %get-tuple-element.11.refs_2_), custom_call_target="tpu_custom_call" | custom-call | tf_op jit(solution)/shard_map/pallas_call | solution.py:500
Async XLA Ops:
  0.6 0.9 copy-start
